TPU v7x, 32 devices: a whole 2x2x4 slice. The times are simulated.
32 devices in a mesh: fsdp: 4 (over z), ep: 8 (over y, x, core).
Axes of the slice: x: 2, y: 2, z: 4, core: 2. Of those that a mesh axis runs over, the one named last changes fastest.
Arguments:
- x_in: bfloat16 [2, 32768, 512], P(None, ('fsdp', 'ep'))
- dy_out: bfloat16 [2, 32768, 512], P(None, ('fsdp', 'ep'))
- expert_idx: int32 [2, 32768, 8], P(None, ('fsdp', 'ep'))
- gate_prob: float32 [2, 32768, 8], P(None, ('fsdp', 'ep'))
- w_one: bfloat16 [64, 512, 256], P('ep', 'fsdp')
- w_two: bfloat16 [64, 256, 512], P('ep', None, 'fsdp')
- w_three: bfloat16 [64, 512, 256], P('ep', 'fsdp')
Outputs:
- output 1: bfloat16 [2, 32768, 512], P(None, ('fsdp', 'ep'))
- output 2: float32 [2, 32768, 8], P(None, ('fsdp', 'ep'))
- output 3: float32 [64, 512, 256], P('ep', 'fsdp')
- output 4: float32 [64, 256, 512], P('ep', None, 'fsdp')
- output 5: float32 [64, 512, 256], P('ep', 'fsdp')
All inputs are finite; a program needn't handle non-finite values.
Results may differ from a plain program's by a relative error of at most 0.001.
Values are sent between devices in bfloat16 or wider.
A program may use at most 1 GiB of HBM per device.

v0:
```python
import jax
import jax.numpy as jnp
from jax import lax
from jax.sharding import PartitionSpec as P


def capacity_of(tok_rows, top_k, experts):
    return 8 * ((5 * tok_rows * top_k + 32 * experts - 1) // (32 * experts))


def route_tables(ids_flat, experts, capacity):
    n_choice = ids_flat.shape[0]
    one_hot = (ids_flat[:, None] == jnp.arange(experts, dtype=jnp.int32)[None, :]).astype(jnp.int32)
    position = jnp.sum((jnp.cumsum(one_hot, axis=0) - one_hot) * one_hot, axis=1)
    choice_slot = jnp.where(position < capacity, ids_flat * capacity + position, experts * capacity)
    holder = jnp.full((experts * capacity + 1,), n_choice, jnp.int32)
    holder = holder.at[choice_slot].set(jnp.arange(n_choice, dtype=jnp.int32))
    return choice_slot, holder[:experts * capacity]


def to_experts(send_buf):
    arrived = lax.all_to_all(send_buf, 'ep', 0, 2, tiled=True)
    return arrived.reshape(arrived.shape[1:])


def from_experts(row_block):
    arrived = lax.all_to_all(row_block[None], 'ep', 2, 0, tiled=True)
    return arrived.reshape((-1,) + arrived.shape[3:])


def expert_pass(x_rows, dy_rows, gate_rows, w_one, w_two, w_three):
    h_one = jnp.einsum('erd,edf->erf', x_rows, w_one, preferred_element_type=jnp.float32)
    h_three = jnp.einsum('erd,edf->erf', x_rows, w_three, preferred_element_type=jnp.float32)
    sigma_one = jax.nn.sigmoid(h_one)
    silu_one = h_one * sigma_one
    act_bf = (silu_one * h_three).astype(jnp.bfloat16)
    y_rows = jnp.einsum('erf,efd->erd', act_bf, w_two, preferred_element_type=jnp.float32)
    dg_rows = jnp.sum(dy_rows.astype(jnp.float32) * y_rows, axis=2)
    g_rows = (gate_rows[:, :, None] * dy_rows).astype(jnp.bfloat16)
    d_act = jnp.einsum('erd,efd->erf', g_rows, w_two, preferred_element_type=jnp.float32)
    dh_three = (d_act * silu_one).astype(jnp.bfloat16)
    dh_one = (d_act * h_three * sigma_one * (1.0 + h_one * (1.0 - sigma_one))).astype(jnp.bfloat16)
    dx_rows = (jnp.einsum('erf,edf->erd', dh_one, w_one, preferred_element_type=jnp.float32) + jnp.einsum('erf,edf->erd', dh_three, w_three, preferred_element_type=jnp.float32)).astype(jnp.bfloat16)
    gw_one = jnp.einsum('erd,erf->edf', x_rows, dh_one, preferred_element_type=jnp.float32)
    gw_two = jnp.einsum('erf,erd->efd', act_bf, g_rows, preferred_element_type=jnp.float32)
    gw_three = jnp.einsum('erd,erf->edf', x_rows, dh_three, preferred_element_type=jnp.float32)
    return dx_rows, dg_rows, (gw_one, gw_two, gw_three)


def solution(mesh):
    ep_size = mesh.shape['ep']
    tok_spec = P(None, ('fsdp', 'ep'), None)
    spec_edf = P('ep', 'fsdp', None)
    spec_efd = P('ep', None, 'fsdp')

    def local_step(x_in, dy_out, expert_idx, gate_prob, w_one, w_two, w_three):
        micro_count, tok_rows, d_model = x_in.shape
        top_k = expert_idx.shape[2]
        local_experts = w_one.shape[0]
        experts = local_experts * ep_size
        capacity = capacity_of(tok_rows, top_k, experts)
        n_choice = tok_rows * top_k
        full_one = lax.all_gather(w_one, 'fsdp', axis=1, tiled=True)
        full_two = lax.all_gather(w_two, 'fsdp', axis=2, tiled=True)
        full_three = lax.all_gather(w_three, 'fsdp', axis=1, tiled=True)
        zero_row = jnp.zeros((1, d_model), x_in.dtype)
        zero_val = jnp.zeros((1,), jnp.float32)
        send_shape = (ep_size, local_experts, capacity)
        dx_parts = []
        dg_parts = []
        grad_sum = None
        for mb_index in range(micro_count):
            choice_slot, holder = route_tables(expert_idx[mb_index].reshape(n_choice), experts, capacity)
            tok_slot = holder // top_k
            x_send = jnp.concatenate([x_in[mb_index], zero_row], axis=0)[tok_slot]
            dy_send = jnp.concatenate([dy_out[mb_index], zero_row], axis=0)[tok_slot]
            gate_send = jnp.concatenate([gate_prob[mb_index].reshape(n_choice), zero_val])[holder]
            x_rows = to_experts(x_send.reshape(send_shape + (d_model,)))
            dy_rows = to_experts(dy_send.reshape(send_shape + (d_model,)))
            gate_rows = to_experts(gate_send.reshape(send_shape))
            dx_rows, dg_rows, grad_part = expert_pass(x_rows, dy_rows, gate_rows, full_one, full_two, full_three)
            dx_back = jnp.concatenate([from_experts(dx_rows), zero_row], axis=0)
            dg_back = jnp.concatenate([from_experts(dg_rows), zero_val])
            picked = dx_back[choice_slot].reshape(tok_rows, top_k, d_model)
            dx_parts.append(jnp.sum(picked.astype(jnp.float32), axis=1).astype(jnp.bfloat16))
            dg_parts.append(dg_back[choice_slot].reshape(tok_rows, top_k))
            if grad_sum is None:
                grad_sum = grad_part
            else:
                grad_sum = tuple(prev_sum + new_part for prev_sum, new_part in zip(grad_sum, grad_part))
        dw_one = lax.psum_scatter(grad_sum[0], 'fsdp', scatter_dimension=1, tiled=True)
        dw_two = lax.psum_scatter(grad_sum[1], 'fsdp', scatter_dimension=2, tiled=True)
        dw_three = lax.psum_scatter(grad_sum[2], 'fsdp', scatter_dimension=1, tiled=True)
        return jnp.stack(dx_parts), jnp.stack(dg_parts), dw_one, dw_two, dw_three

    return jax.shard_map(local_step, mesh=mesh, in_specs=(tok_spec, tok_spec, tok_spec, tok_spec, spec_edf, spec_efd, spec_edf), out_specs=(tok_spec, tok_spec, spec_edf, spec_efd, spec_edf), check_vma=False)
```

profile of v0, /device:TPU:0, one launch (start us, length us, event | category | flops | bytes accessed | tf_op | source)
XLA Modules:
  0.0 1376.2 jit_solution(10454085551893157215)
XLA Ops:
  12.0 34.0 %reduce-window.14 = s32[64,64,128]{2,1,0:T(8,128)S(1)} reduce-window(s32[64,64,128]{2,1,0:T(8,128)} %fusion.14, s32[]{:T(128)} %constant.41.clone.1), window={size=1x1x128 pad=0_0x0_0x127_0}, to_apply=%region_0.0 | reduce-window | flops 66584576 | bytes 4194308 | tf_op jit(solution)/shard_map/reduce-window
  48.6 1.9 fusion.13
  50.6 30.5 %scatter_custom_fusion = s32[10241]{0:T(1024)S(1)} fusion(s32[8192]{0:T(1024)S(1)} %bitcast.190, s32[8192]{0:T(1024)S(1)} %iota.19, s32[]{:T(128)} %constant.40.clone.1), kind=kCustom, calls=%fused_computation.97 | custom fusion | bytes 40968 | tf_op jit(solution)/shard_map/scatter | solution.py:17
  81.1 56.8 %gather_fusion = f32[10240]{0:T(1024)S(1)} fusion(f32[8193]{0:T(1024)S(1)} %pad_maximum_fusion.5, s32[10240]{0:T(1024)S(1)} %get-tuple-element.31), kind=kCustom, calls=%fused_computation | custom fusion | bytes 122880 | tf_op jit(solution)/shard_map/gather | solution.py:77
  138.6 5.4 all-to-all-start
  147.3 34.0 %reduce-window.16 = s32[64,64,128]{2,1,0:T(8,128)S(1)} reduce-window(s32[64,64,128]{2,1,0:T(8,128)} %fusion.15, s32[]{:T(128)} %constant.41.clone.1), window={size=1x1x128 pad=0_0x0_0x127_0}, to_apply=%region_5.6 | reduce-window | flops 66584576 | bytes 4194308 | tf_op jit(solution)/shard_map/reduce-window.2
  186.5 30.5 %scatter_custom_fusion.1 = s32[10241]{0:T(1024)S(1)} fusion(s32[8192]{0:T(1024)S(1)} %bitcast.192, s32[8192]{0:T(1024)S(1)} %iota.20, s32[]{:T(128)} %constant.40.clone.1), kind=kCustom, calls=%fused_computation.95 | custom fusion | bytes 40968 | tf_op jit(solution)/shard_map/scatter | solution.py:17
  217.0 56.8 %gather_fusion.4 = f32[10240]{0:T(1024)S(1)} fusion(f32[8193]{0:T(1024)S(1)} %pad_maximum_fusion.4, s32[10240]{0:T(1024)S(1)} %get-tuple-element.33), kind=kCustom, calls=%fused_computation.4 | custom fusion | bytes 122880 | tf_op jit(solution)/shard_map/gather | solution.py:77
  274.5 4.2 all-to-all-start.4
  280.5 41.8 %gather_fusion.6 = bf16[10240,512]{1,0:T(8,128)(2,1)} fusion(bf16[1025,512]{1,0:T(8,128)(2,1)S(1)} %concatenate.36, s32[10240]{0:T(1024)S(1)} %get-tuple-element.34), kind=kCustom, calls=%fused_computation.6 | custom fusion | bytes 21012480 | tf_op jit(solution)/shard_map/gather | solution.py:75
  322.2 5.1 all-to-all-start.6
  329.1 41.7 %gather_fusion.1 = bf16[10240,512]{1,0:T(8,128)(2,1)} fusion(bf16[1025,512]{1,0:T(8,128)(2,1)S(1)} %concatenate.31, s32[10240]{0:T(1024)S(1)} %get-tuple-element.32), kind=kCustom, calls=%fused_computation.1 | custom fusion | bytes 21012480 | tf_op jit(solution)/shard_map/gather | solution.py:76
  370.8 73.0 %all-to-all-done.6 = bf16[8,8,160,512]{3,2,1,0:T(8,128)(2,1)} async-done(((bf16[8,8,160,512]{3,2,1,0:T(8,128)(2,1)}), bf16[8,8,160,512]{3,2,1,0:T(8,128)(2,1)}, u32[]{:S(2)}, u32[]{:S(2)}) %all-to-all-start.6) | async-done | bytes 10485792 | tf_op jit(solution)/shard_map/all_to_all | solution.py:22
  443.9 5.1 all-to-all-start.1
  449.1 41.7 %gather_fusion.2 = bf16[10240,512]{1,0:T(8,128)(2,1)} fusion(bf16[1025,512]{1,0:T(8,128)(2,1)S(1)} %concatenate.32, s32[10240]{0:T(1024)S(1)} %get-tuple-element.32), kind=kCustom, calls=%fused_computation.2 | custom fusion | bytes 21012480 | tf_op jit(solution)/shard_map/gather | solution.py:75
  490.8 74.7 %all-to-all-done.1 = bf16[8,8,160,512]{3,2,1,0:T(8,128)(2,1)} async-done(((bf16[8,8,160,512]{3,2,1,0:T(8,128)(2,1)}), bf16[8,8,160,512]{3,2,1,0:T(8,128)(2,1)}, u32[]{:S(2)}, u32[]{:S(2)}) %all-to-all-start.1) | async-done | bytes 10485792 | tf_op jit(solution)/shard_map/all_to_all | solution.py:22
  565.5 5.2 all-to-all-start.2
  572.2 41.7 %gather_fusion.5 = bf16[10240,512]{1,0:T(8,128)(2,1)} fusion(bf16[1025,512]{1,0:T(8,128)(2,1)S(1)} %concatenate.35, s32[10240]{0:T(1024)S(1)} %get-tuple-element.34), kind=kCustom, calls=%fused_computation.5 | custom fusion | bytes 21012480 | tf_op jit(solution)/shard_map/gather | solution.py:76
  613.9 73.2 %all-to-all-done.2 = bf16[8,8,160,512]{3,2,1,0:T(8,128)(2,1)} async-done(((bf16[8,8,160,512]{3,2,1,0:T(8,128)(2,1)}), bf16[8,8,160,512]{3,2,1,0:T(8,128)(2,1)}, u32[]{:S(2)}, u32[]{:S(2)}) %all-to-all-start.2) | async-done | bytes 10485792 | tf_op jit(solution)/shard_map/all_to_all | solution.py:22
  687.1 5.2 all-to-all-start.5
  693.6 9.2 copy.133
  702.8 9.1 copy.124
  711.9 14.0 %bitcast_convert_fusion.1 = f32[8,1,8,160,512]{4,3,0,2,1:T(8,128)} fusion(bf16[8,8,160,512]{3,2,1,0:T(8,128)(2,1)} %all-to-all-done.1), kind=kLoop, calls=%fused_computation.21 | loop fusion | flops 5242880 | bytes 31457280 | tf_op jit(solution)/shard_map/convert_element_type | solution.py:39
  725.9 21.9 %copy.137 = f32[8,1280,512]{1,2,0:T(8,128)} copy(f32[8,1280,512]{2,1,0:T(8,128)} %bitcast.152) | data formatting | bytes 41943040 | tf_op jit(solution)/shard_map/convert_element_type | solution.py:39
  747.7 11.4 fusion.30
  759.2 12.4 fusion.5
  771.6 17.8 %multiply_convert_fusion.3 = (bf16[8,1280,256]{2,1,0:T(8,128)(2,1)}, bf16[8,1280,256]{2,1,0:T(8,128)(2,1)}, bf16[8,1280,256]{2,1,0:T(8,128)(2,1)}) fusion(f32[8,1280,256]{2,1,0:T(8,128)} %fusion.30, f32[8,1280,256]{2,1,0:T(8,128)} %fusion.5, bf16[8,1280,512]{2,1,0:T(8,128)(2,1)} %bitcast.163, bf16[8,512,256]{2,1,0:T(8,128)(2,1)} %all-gather.6.cloned.1.call-done), kind=kOutput, calls=%fused_computation.23 | convolution fusion | flops 2723676160 | bytes 49283072 | tf_op jit(solution)/shard_map/erd,edf->erf/dot_general | solution.py:33
  789.4 10.8 fusion.35
  800.2 8.6 all-to-all-done.5
  808.8 13.9 %bitcast_convert_fusion = f32[8,1,8,160,512]{4,3,0,2,1:T(8,128)} fusion(bf16[8,8,160,512]{3,2,1,0:T(8,128)(2,1)} %all-to-all-done.5), kind=kLoop, calls=%fused_computation.20 | loop fusion | flops 5242880 | bytes 31457280 | tf_op jit(solution)/shard_map/convert_element_type | solution.py:39
  822.7 22.0 %copy.142 = f32[8,1280,512]{1,2,0:T(8,128)} copy(f32[8,1280,512]{2,1,0:T(8,128)} %bitcast.155) | data formatting | bytes 41943040 | tf_op jit(solution)/shard_map/convert_element_type | solution.py:39
  844.8 11.0 fusion.32
  855.7 11.8 fusion.7
  867.5 17.5 %multiply_convert_fusion.2 = (bf16[8,1280,256]{2,1,0:T(8,128)(2,1)}, bf16[8,1280,256]{2,1,0:T(8,128)(2,1)}, bf16[8,1280,256]{2,1,0:T(8,128)(2,1)}) fusion(f32[8,1280,256]{2,1,0:T(8,128)} %fusion.32, f32[8,1280,256]{2,1,0:T(8,128)} %fusion.7, bf16[8,1280,512]{2,1,0:T(8,128)(2,1)} %bitcast.159, bf16[8,512,256]{2,1,0:T(8,128)(2,1)} %all-gather.6.cloned.1.call-done), kind=kOutput, calls=%fused_computation.22 | convolution fusion | flops 2723676160 | bytes 49283072 | tf_op jit(solution)/shard_map/erd,edf->erf/dot_general | solution.py:33
  885.0 12.0 convolution_add_fusion
  897.1 10.7 multiply_reduce_fusion.1
  908.7 6.0 reduce.8
  915.7 3.6 all-to-all-start.8
  919.3 10.7 multiply_reduce_fusion
  930.0 11.2 fusion.33
  941.6 6.0 reduce.6
  948.6 4.2 all-to-all-start.9
  952.8 14.8 %fusion.1 = bf16[1,8,1280,512]{3,2,1,0:T(8,128)(2,1)} fusion(f32[8,1280,512]{2,1,0:T(8,128)} %fusion.33, bf16[8,1280,256]{2,1,0:T(8,128)(2,1)} %get-tuple-element.20, bf16[8,512,256]{2,1,0:T(8,128)(2,1)} %all-gather.6.cloned.1.call-done), kind=kOutput, calls=%fused_computation.19 | convolution fusion | flops 2694840320 | bytes 38797312 | tf_op jit(solution)/shard_map/erf,edf->erd/dot_general | solution.py:43
  967.5 12.4 copy.134
  979.9 5.2 all-to-all-start.7
  985.6 10.9 fusion.34
  996.4 12.0 convolution_add_fusion.1
  1008.5 11.2 fusion.31
  1019.7 14.7 %fusion = bf16[1,8,1280,512]{3,2,1,0:T(8,128)(2,1)} fusion(f32[8,1280,512]{2,1,0:T(8,128)} %fusion.31, bf16[8,1280,256]{2,1,0:T(8,128)(2,1)} %get-tuple-element.17, bf16[8,512,256]{2,1,0:T(8,128)(2,1)} %all-gather.6.cloned.1.call-done), kind=kOutput, calls=%fused_computation.18 | convolution fusion | flops 2694840320 | bytes 38797312 | tf_op jit(solution)/shard_map/erf,edf->erd/dot_general | solution.py:43
  1034.4 12.4 copy.125
  1046.8 54.8 %all-to-all-done.7 = bf16[1,8,1280,512]{3,1,0,2:T(8,128)(2,1)} async-done(((bf16[1,8,1280,512]{3,1,0,2:T(8,128)(2,1)}), bf16[1,8,1280,512]{3,1,0,2:T(8,128)(2,1)}, u32[]{:S(2)}, u32[]{:S(2)}) %all-to-all-start.7) | async-done | bytes 10485792 | tf_op jit(solution)/shard_map/all_to_all | solution.py:27
  1101.6 5.1 all-to-all-start.3
  1107.0 10.3 fusion.4
  1117.3 12.4 fusion.16
  1134.2 45.5 %gather_fusion.8 = f32[8192]{0:T(1024)S(1)} fusion(f32[10241]{0:T(1024)S(1)} %get-tuple-element.36, s32[8192]{0:T(1024)S(1)} %broadcast_clamp_fusion.1), kind=kCustom, calls=%fused_computation.8 | custom fusion | bytes 98304 | tf_op jit(solution)/shard_map/gather | solution.py:86
  1180.2 45.5 %gather_fusion.9 = f32[8192]{0:T(1024)S(1)} fusion(f32[10241]{0:T(1024)S(1)} %get-tuple-element.35, s32[8192]{0:T(1024)S(1)} %broadcast_clamp_fusion), kind=kCustom, calls=%fused_computation.9 | custom fusion | bytes 98304 | tf_op jit(solution)/shard_map/gather | solution.py:86
  1226.8 11.9 copy.135
  1238.7 10.0 concatenate.37
  1248.8 39.3 %gather_fusion.7 = bf16[8192,512]{1,0:T(8,128)(2,1)} fusion(bf16[10241,512]{1,0:T(8,128)(2,1)} %concatenate.37, s32[8192]{0:T(1024)S(1)} %broadcast_clamp_fusion), kind=kCustom, calls=%fused_computation.7 | custom fusion | bytes 16809984 | tf_op jit(solution)/shard_map/gather | solution.py:84
  1288.1 11.9 copy.126
  1300.0 9.8 concatenate.33
  1309.8 39.5 %gather_fusion.3 = bf16[8192,512]{1,0:T(8,128)(2,1)} fusion(bf16[10241,512]{1,0:T(8,128)(2,1)} %concatenate.33, s32[8192]{0:T(1024)S(1)} %broadcast_clamp_fusion.1), kind=kCustom, calls=%fused_computation.3 | custom fusion | bytes 16809984 | tf_op jit(solution)/shard_map/gather | solution.py:84
  1349.3 9.0 bitcast_reduce_fusion
  1358.4 9.0 bitcast_reduce_fusion.1
  (112 shorter events, 35.0 us)
Async XLA Ops:
  50.5 30.6 %copy-start.6 = (s32[8192,1]{0,1:T(1,128)}, s32[8192,1]{0,1:T(1,128)S(1)}, u32[]{:S(2)}) copy-start(s32[8192,1]{0,1:T(1,128)S(1)} %compare_select_fusion.1) | copy-start | bytes 98308
  138.6 135.9 %all-to-all-start = ((f32[8,8,160]{2,1,0:T(8,128)}), f32[8,8,160]{2,1,0:T(8,128)S(1)}, u32[]{:S(2)}, u32[]{:S(2)}) async-start(f32[8,8,160]{2,1,0:T(8,128)} %reshape.177), calls=%async_computation | async-start | bytes 131072 | tf_op jit(solution)/shard_map/all_to_all | solution.py:22
  185.9 0.6 copy-start.8
  274.5 47.7 %all-to-all-start.4 = ((f32[8,8,160]{2,1,0:T(8,128)}), f32[8,8,160]{2,1,0:T(8,128)S(1)}, u32[]{:S(2)}, u32[]{:S(2)}) async-start(f32[8,8,160]{2,1,0:T(8,128)} %reshape.184), calls=%async_computation.4 | async-start | bytes 131072 | tf_op jit(solution)/shard_map/all_to_all | solution.py:22
  322.2 121.6 %all-to-all-start.6 = ((bf16[8,8,160,512]{3,2,1,0:T(8,128)(2,1)}), bf16[8,8,160,512]{3,2,1,0:T(8,128)(2,1)}, u32[]{:S(2)}, u32[]{:S(2)}) async-start(bf16[8,8,160,512]{3,2,1,0:T(8,128)(2,1)} %bitcast.170), calls=%async_computation.6 | async-start | bytes 20971520 | tf_op jit(solution)/shard_map/all_to_all | solution.py:22
  443.9 121.6 %all-to-all-start.1 = ((bf16[8,8,160,512]{3,2,1,0:T(8,128)(2,1)}), bf16[8,8,160,512]{3,2,1,0:T(8,128)(2,1)}, u32[]{:S(2)}, u32[]{:S(2)}) async-start(bf16[8,8,160,512]{3,2,1,0:T(8,128)(2,1)} %bitcast.171), calls=%async_computation.1 | async-start | bytes 20971520 | tf_op jit(solution)/shard_map/all_to_all | solution.py:22
  565.5 121.6 %all-to-all-start.2 = ((bf16[8,8,160,512]{3,2,1,0:T(8,128)(2,1)}), bf16[8,8,160,512]{3,2,1,0:T(8,128)(2,1)}, u32[]{:S(2)}, u32[]{:S(2)}) async-start(bf16[8,8,160,512]{3,2,1,0:T(8,128)(2,1)} %bitcast.169), calls=%async_computation.2 | async-start | bytes 20971520 | tf_op jit(solution)/shard_map/all_to_all | solution.py:22
  570.6 177.1 %all-gather.8.cloned.1.call-start = ((), (), s32[]{:S(2)}) async-start(), calls=%async_computation.15 | async-start | bytes 2621440 | tf_op jit(solution)/shard_map/all_gather | solution.py:63
  571.4 187.8 %all-gather.4.cloned.1.call-start = ((), (), s32[]{:S(2)}) async-start(), calls=%async_computation.13 | async-start | bytes 2621440 | tf_op jit(solution)/shard_map/all_gather | solution.py:64
  687.1 121.7 %all-to-all-start.5 = ((bf16[8,8,160,512]{3,2,1,0:T(8,128)(2,1)}), bf16[8,8,160,512]{3,2,1,0:T(8,128)(2,1)}, u32[]{:S(2)}, u32[]{:S(2)}) async-start(bf16[8,8,160,512]{3,2,1,0:T(8,128)(2,1)} %bitcast.168), calls=%async_computation.5 | async-start | bytes 20971520 | tf_op jit(solution)/shard_map/all_to_all | solution.py:22
  692.3 79.3 %all-gather.6.cloned.1.call-start = ((), (), s32[]{:S(2)}) async-start(), calls=%async_computation.14 | async-start | bytes 2621440 | tf_op jit(solution)/shard_map/all_gather | solution.py:65
  693.0 675.9 %reduce-scatter.8.cloned.1.call-start = ((), (), s32[]{:S(2)}) async-start(), calls=%async_computation.18 | async-start | bytes 5242880 | tf_op jit(solution)/shard_map/reduce_scatter | solution.py:93
  693.4 65.8 %copy-start.2 = (f32[8,1280]{1,0:T(8,128)}, f32[8,1280]{1,0:T(8,128)S(1)}, u32[]{:S(2)}) copy-start(f32[8,1280]{1,0:T(8,128)S(1)} %mul.103) | copy-start | bytes 122884
  693.5 162.2 %copy-start.4 = (f32[8,1280]{1,0:T(8,128)}, f32[8,1280]{1,0:T(8,128)S(1)}, u32[]{:S(2)}) copy-start(f32[8,1280]{1,0:T(8,128)S(1)} %mul.115) | copy-start | bytes 122884
  822.7 22.0 %copy-start = (bf16[8,512,256]{2,1,0:T(8,128)(2,1)S(1)}, bf16[8,512,256]{2,1,0:T(8,128)(2,1)}, u32[]{:S(2)}) copy-start(bf16[8,512,256]{2,1,0:T(8,128)(2,1)} %all-gather.8.cloned.1.call-done) | copy-start | bytes 6291460
  844.8 11.0 copy-start.1
  915.7 32.9 %all-to-all-start.8 = ((f32[8,1,1280]{2,1,0:T(1,128)}), f32[8,1,1280]{2,1,0:T(1,128)S(1)}, u32[]{:S(2)}, u32[]{:S(2)}) async-start(f32[8,1,1280]{2,1,0:T(1,128)} %reshape.306), calls=%async_computation.8 | async-start | bytes 81920 | tf_op jit(solution)/shard_map/all_to_all | solution.py:27
  948.6 31.3 %all-to-all-start.9 = ((f32[8,1,1280]{2,1,0:T(1,128)}), f32[8,1,1280]{2,1,0:T(1,128)S(1)}, u32[]{:S(2)}, u32[]{:S(2)}) async-start(f32[8,1,1280]{2,1,0:T(1,128)} %reshape.304), calls=%async_computation.9 | async-start | bytes 81920 | tf_op jit(solution)/shard_map/all_to_all | solution.py:27
  979.9 121.7 %all-to-all-start.7 = ((bf16[1,8,1280,512]{3,1,0,2:T(8,128)(2,1)}), bf16[1,8,1280,512]{3,1,0,2:T(8,128)(2,1)}, u32[]{:S(2)}, u32[]{:S(2)}) async-start(bf16[1,8,1280,512]{3,1,0,2:T(8,128)(2,1)} %copy.134), calls=%async_computation.7 | async-start | bytes 20971520 | tf_op jit(solution)/shard_map/all_to_all | solution.py:27
  985.1 383.8 %reduce-scatter.4.cloned.1.call-start = ((), (), s32[]{:S(2)}) async-start(), calls=%async_computation.16 | async-start | bytes 5242880 | tf_op jit(solution)/shard_map/reduce_scatter | solution.py:91
  1046.8 60.2 %copy-start.3 = (f32[8,1280]{1,0:T(8,128)S(1)}, f32[8,1280]{1,0:T(8,128)}, u32[]{:S(2)}) copy-start(f32[8,1280]{1,0:T(8,128)} %copy-done.2) | copy-start | bytes 122884
  1101.6 186.5 %all-to-all-start.3 = ((bf16[1,8,1280,512]{3,1,0,2:T(8,128)(2,1)}), bf16[1,8,1280,512]{3,1,0,2:T(8,128)(2,1)}, u32[]{:S(2)}, u32[]{:S(2)}) async-start(bf16[1,8,1280,512]{3,1,0,2:T(8,128)(2,1)} %copy.125), calls=%async_computation.3 | async-start | bytes 20971520 | tf_op jit(solution)/shard_map/all_to_all | solution.py:27
  1106.7 10.5 copy-start.5
  1106.7 262.2 %reduce-scatter.6.cloned.1.call-start = ((), (), s32[]{:S(2)}) async-start(), calls=%async_computation.17 | async-start | bytes 5242880 | tf_op jit(solution)/shard_map/reduce_scatter | solution.py:92
  1117.3 12.5 copy-start.7
  1117.3 12.5 copy-start.9
Sparse Core Ops, SparseCore 0:
  573.0 46.8 all-gather.7
  621.5 46.1 all-gather.3
  694.7 46.8 all-gather.5
  897.2 76.0 reduce-scatter.7
  1008.6 78.3 reduce-scatter.3
  1129.9 78.2 reduce-scatter.5
where the time goes:
time: 1390 us; the launch traced here: 1380 us
  local copies, waits for them, and re-layouts  662 us (48%)
  waiting for transfers between devices  286 us (21%)
  matrix products  224 us (16%)
  other arithmetic  139 us (10%)
  starting transfers between devices  49.3 us (4%)
  between operations  15.2 us (1%)
    all_to_all x6, waiting for transfers between devices, to_experts(): arrived = lax.all_to_all(send_buf, 'ep', 0, 2, tiled=True)  230 us
    gather x2, local copies, waits for them, and re-layouts, local_step(): jnp.concatenate([gate_prob[mb_index].reshape(n_choice), zero_val])[holder]  114 us
    gather x2, local copies, waits for them, and re-layouts, local_step(): dg_parts.append(dg_back[choice_slot].reshape(tok_rows, top_k))  91.1 us
    gather x2, local copies, waits for them, and re-layouts, local_step(): x_send = jnp.concatenate([x_in[mb_index], zero_row], axis=0)[tok_slot]  83.4 us
    gather x2, local copies, waits for them, and re-layouts, local_step(): dy_send = jnp.concatenate([dy_out[mb_index], zero_row], axis=0)[tok_slot]  83.4 us
    gather x2, local copies, waits for them, and re-layouts, local_step(): picked = dx_back[choice_slot].reshape(tok_rows, top_k, d_model)  78.8 us
    another operation x6, other arithmetic  69.8 us
    scatter x2, local copies, waits for them, and re-layouts, route_tables(): holder = holder.at[choice_slot].set(jnp.arange(n_choice, dtype=jnp.int32))  60.9 us
  transfers between devices with their start and end apart: 16, of which 5 were waited for; matrix products, arithmetic and copies ran while one was open for 58% of the time, Pallas kernels for 0%

commit v1 on v0

v1 whole, which is shorter than its diff:
```python
import functools

import jax
import jax.numpy as jnp
from jax import lax
from jax.experimental import pallas as pl
from jax.experimental.pallas import tpu as pltpu
from jax.sharding import PartitionSpec as P

MESH = pl.DeviceIdType.MESH
BF = jnp.bfloat16
F32 = jnp.float32
ANY = pl.BlockSpec(memory_space=pl.ANY)
VM = pl.BlockSpec(memory_space=pltpu.VMEM)
VLIM = 62 * 1024 * 1024
GROUPS = (1, 3, 4)
DROPPED = -4096.0
LANES = 128
EXP = 8
NT = (((1,), (1,)), ((), ()))
TN = (((0,), (0,)), ((), ()))


def params(collective_id=None):
    if collective_id is None:
        return pltpu.CompilerParams(vmem_limit_bytes=VLIM)
    return pltpu.CompilerParams(collective_id=collective_id, has_side_effects=True, vmem_limit_bytes=VLIM)


def cost(gflop, mbytes):
    return pl.CostEstimate(flops=gflop * 10**9, bytes_accessed=mbytes * 10**6, transcendentals=0)


def capacity_of(tok_rows, top_k, experts):
    return 8 * ((5 * tok_rows * top_k + 32 * experts - 1) // (32 * experts))


def dot(a, b):
    return jnp.dot(a, b, preferred_element_type=F32)


def hot_bf(sel):
    return jnp.where(sel, 1.0, 0.0).astype(BF)


def iota(shape, dim):
    return lax.broadcasted_iota(jnp.int32, shape, dim).astype(F32)


class Place:
    def __init__(self):
        me = lax.axis_index('ep')
        z = lax.axis_index('fsdp')
        self.me = me
        self.core = lax.rem(me, 2)
        self.other = 1 - self.core
        self.partner = me + 1 - 2 * self.core
        self.chip = lax.div(me, 2)
        self.to_x = 1 - 2 * lax.rem(self.chip, 2)
        self.to_y = 2 - 4 * lax.div(self.chip, 2)
        self.chip_x = self.chip + self.to_x
        self.chip_y = self.chip + self.to_y
        self.chip_d = self.chip_x + self.to_y
        self.dev_x = (z, 2 * self.chip_x + self.core)
        self.dev_y = (z, 2 * self.chip_y + self.core)
        self.dev_c = (z, self.partner)

    def greet(self):
        barrier = pltpu.get_barrier_semaphore()
        devices = (self.dev_x, self.dev_y, self.dev_c)
        for dev in devices:
            pl.semaphore_signal(barrier, inc=1, device_id=dev, device_id_type=MESH)
        pl.semaphore_wait(barrier, len(devices))


def rcopy(src, dst, sems, i, dev):
    return pltpu.make_async_remote_copy(src_ref=src, dst_ref=dst, send_sem=sems[0].at[i], recv_sem=sems[1].at[i], device_id=dev, device_id_type=MESH)


def arrive(ref, sems, i, dev):
    rcopy(ref, ref, sems, i, dev).wait_recv()


def gather_rows_kernel(capacity, x_ref, dy_ref, meta_ref, rows, pos_ref, gate_ref, post_ref, ids_ref, tg, mg, hot_a, hot_b, tri, stage, s_x, r_x, s_y, r_y, s_c, r_c, s_ax, r_ax, s_ay, r_ay, s_fx, r_fx, s_fy, r_fy, s_fa, r_fa, s_fb, r_fb, s_l, s_s):
    at = Place()
    tok = x_ref.shape[1]
    half = tok // 2
    by_x, by_y, by_c, relay_x, relay_y = (s_x, r_x), (s_y, r_y), (s_c, r_c), (s_ax, r_ax), (s_ay, r_ay)
    fwd_x, fwd_y, fwd_a, fwd_b = (s_fx, r_fx), (s_fy, r_fy), (s_fa, r_fa), (s_fb, r_fb)
    chunks = range(5)

    def slot_of(core, chip):
        return core * 4 + chip

    def own(k):
        if k == 0:
            return meta_ref
        return (dy_ref, x_ref)[k % 2].at[(k - 1) // 2]

    def block(k, slot):
        if k == 0:
            return mg.at[slot]
        return tg.at[(k - 1) % 2, slot, (k - 1) // 2]

    def part(k, slot, h):
        if k == 0:
            return mg.at[slot, h]
        return block(k, slot).at[pl.ds(h * half, half)]

    slot = slot_of(at.core, at.chip)
    slot_x = slot_of(at.core, at.chip_x)
    slot_y = slot_of(at.core, at.chip_y)
    slot_d = slot_of(at.core, at.chip_d)

    def side_hops(k):
        return (
            (part(k, slot_x, 0), part(k, slot_x, 0), relay_y, k, at.dev_y),
            (block(k, slot_x), block(k, slot_x), fwd_x, k, at.dev_c),
            (part(k, slot_y, 1), part(k, slot_y, 1), relay_x, k, at.dev_x),
            (block(k, slot_y), block(k, slot_y), fwd_y, k, at.dev_c),
        )

    def corner_hops(k):
        return ((part(k, slot_d, 0), part(k, slot_d, 0), fwd_a, k, at.dev_c), (part(k, slot_d, 1), part(k, slot_d, 1), fwd_b, k, at.dev_c))

    def own_hops(k):
        return tuple((own(k), block(k, slot), sems, k, dev) for sems, dev in ((by_x, at.dev_x), (by_y, at.dev_y), (by_c, at.dev_c)))

    def send(hops):
        for hop in hops:
            rcopy(*hop).start()

    def pass_on(k):
        hops = side_hops(k)
        arrive(block(k, slot_x), by_x, k, at.dev_x)
        send(hops[:2])
        arrive(block(k, slot_y), by_y, k, at.dev_y)
        send(hops[2:])
        arrive(block(k, slot_of(at.other, at.chip_x)), fwd_x, k, at.dev_c)
        arrive(block(k, slot_of(at.other, at.chip_y)), fwd_y, k, at.dev_c)

    def pass_on_corner(k):
        hops = corner_hops(k)
        far = slot_of(at.other, at.chip_d)
        arrive(part(k, slot_d, 0), relay_y, k, at.dev_y)
        send(hops[:1])
        arrive(part(k, slot_d, 1), relay_x, k, at.dev_x)
        send(hops[1:])
        arrive(part(k, far, 0), fwd_a, k, at.dev_c)
        arrive(part(k, far, 1), fwd_b, k, at.dev_c)

    local = [pltpu.make_async_copy(own(k), block(k, slot), s_l.at[k]) for k in chunks]
    for copy in local:
        copy.start()
    at.greet()
    for k in chunks:
        send(own_hops(k)[:2])
    for k in chunks:
        send(own_hops(k)[2:])

    tri[...] = hot_bf(iota((tok, tok), 0) < iota((tok, tok), 1))
    for copy in local:
        copy.wait()
    arrive(block(0, slot_of(at.other, at.chip)), by_c, 0, at.dev_c)
    pass_on(0)
    pass_on_corner(0)
    sub = iota((EXP, tok), 0)

    def hot_of(src, mb, device):
        ids = mg[src, 0, mb]
        vals = mg[src, 1, mb]
        want = sub + (device * EXP).astype(F32)
        hot = jnp.zeros((EXP, tok), F32)
        gate = hot
        for j in range(ids.shape[0]):
            sel = ids[j:j + 1, :] == want
            hot = jnp.where(sel, 1.0, hot)
            gate = jnp.where(sel, vals[j:j + 1, :], gate)
        return hot, gate

    @pl.loop(0, 16)
    def _(i):
        hot, gate = hot_of(lax.div(i, 2), lax.rem(i, 2), at.me)
        hot_a[pl.ds(pl.multiple_of(i * EXP, EXP), EXP), :] = hot
        gate_ref[i] = gate

    @pl.loop(0, 8)
    def _(i):
        src, mb = slot_of(at.core, lax.div(i, 2)), lax.rem(i, 2)
        row = pl.multiple_of(i * 2 * EXP, EXP)
        hot_b[pl.ds(row, EXP), :] = hot_of(src, mb, at.me)[0]
        hot_b[pl.ds(row + EXP, EXP), :] = hot_of(src, mb, at.partner)[0]
        ids_ref[i] = mg[src, 0, mb]

    def place_of(hot):
        before = dot(hot.astype(BF), tri[...])
        keep = jnp.logical_and(hot > 0.5, before < capacity)
        return jnp.where(keep, before, DROPPED)

    pos_ref[...] = place_of(hot_a[...]).reshape(pos_ref.shape)
    post_ref[...] = jnp.transpose(place_of(hot_b[...]))

    place = iota((capacity, tok), 0)
    per = EXP // 2

    def stored(b, kind, i):
        return pltpu.make_async_copy(stage.at[b], rows.at[kind, :, i], s_s.at[b])

    @pl.loop(0, 32)
    def _(t):
        u = lax.div(t, 8)
        first = lax.div((3 - u) * (2 - u) * (1 - u), 6)
        last = lax.div(u * (u - 1) * (u - 2), 6)
        sides = 1 - first - last

        @pl.when(t == 0)
        def _():
            for k in chunks[1:]:
                arrive(block(k, slot_of(at.other, at.chip)), by_c, k, at.dev_c)

        for k in chunks[1:]:

            @pl.when(t == 4 + 4 * k)
            def _():
                pass_on(k)

            @pl.when(t == 22 + 2 * k)
            def _():
                pass_on_corner(k)

        k0 = first * lax.div(t, 2) + sides * (lax.div(t, 4) - 2) + last * (lax.div(t, 2) - 12)
        kind, mb = lax.rem(k0, 2), lax.div(k0, 2)
        far = (first + last) * lax.rem(t, 2) + sides * lax.div(lax.rem(t, 4), 2)
        core = at.core + far * (1 - 2 * at.core)
        odd = lax.rem(t, 2)
        chip = at.chip + sides * ((1 - odd) * at.to_x + odd * at.to_y) + last * (at.to_x + at.to_y)
        src = slot_of(core, chip)
        i = src * 2 + mb
        b = lax.rem(t, 2)

        @pl.when(t >= 2)
        def _():
            stored(b, kind, i).wait()

        pos = pos_ref[i]
        for h in range(0, EXP, per):
            hot = jnp.concatenate([hot_bf(pos[e:e + 1, :] == place) for e in range(h, h + per)], axis=0)
            stage[b, h:h + per] = dot(hot, tg[kind, src, mb]).astype(BF).reshape(per, capacity, -1)
        stored(b, kind, i).start()

    for b in range(2):
        stored(b, 0, b).wait()
    for k in chunks:
        for hop in own_hops(k) + side_hops(k) + corner_hops(k):
            rcopy(*hop).wait_send()


def gather_rows(x_in, dy_out, meta, capacity):
    micro, tok, width = x_in.shape
    dma = pltpu.SemaphoreType.DMA
    table = jax.ShapeDtypeStruct((16, EXP, tok), F32)
    hots = pltpu.VMEM((LANES, tok), F32)
    return pl.pallas_call(
        functools.partial(gather_rows_kernel, capacity),
        out_shape=(jax.ShapeDtypeStruct((2, EXP, 16, capacity, width), BF), table, table, jax.ShapeDtypeStruct((tok, LANES), F32), jax.ShapeDtypeStruct((8, EXP, tok), F32)),
        in_specs=[ANY] * 3,
        out_specs=(ANY, VM, VM, VM, VM),
        scratch_shapes=[pltpu.VMEM((2, 8, micro, tok, width), BF), pltpu.VMEM((8,) + meta.shape, F32), hots, hots, pltpu.VMEM((tok, tok), BF), pltpu.VMEM((2, EXP, capacity, width), BF)] + [dma((5,))] * 19 + [dma((2,))],
        name='gather_rows',
        compiler_params=params(0),
        cost_estimate=cost(100, 80),
    )(x_in, dy_out, meta)


def expert_kernel(first, pos_ref, gate_ref, xr_ref, dyr_ref, wa_ref, dxr_ref, dg_ref, gw_ref, acc13, acc2):
    m = pl.program_id(1)
    e = pl.program_id(0) + first
    blocks, capacity, width = xr_ref.shape[2:]
    tok = pos_ref.shape[2]
    rows = blocks * capacity
    x = xr_ref[0, 0].reshape(rows, width)
    dy = dyr_ref[0, 0].reshape(rows, width)
    folds = [wa_ref[:, c // 2, 0, LANES * (c % 2):LANES * (c % 2) + LANES].reshape(width, LANES) for c in range(4)]
    w13 = jnp.concatenate(folds, axis=1)
    w2 = jnp.concatenate([wa_ref[z, 2, 0] for z in range(4)], axis=1)
    ff = w2.shape[0]
    place = iota((capacity, tok), 0)
    pos_rows = [pos_ref[m * blocks + b, pl.ds(e, 1), :] for b in range(blocks)]
    q = jnp.concatenate([jnp.sum(jnp.where(pos_rows[b] == place, gate_ref[m * blocks + b, pl.ds(e, 1), :], 0.0), axis=1, keepdims=True) for b in range(blocks)], axis=0)
    g = (q * dy.astype(F32)).astype(BF)
    h = dot(x, w13)
    dyw = lax.dot_general(dy, w2, NT, preferred_element_type=F32)
    da = lax.dot_general(g, w2, NT, preferred_element_type=F32)
    h1 = h[:, :ff]
    h3 = h[:, ff:]
    sig = jax.nn.sigmoid(h1)
    s = h1 * sig
    act = (s * h3).astype(BF)
    dg = jnp.sum(act.astype(F32) * dyw, axis=1, keepdims=True)
    dh3 = (da * s).astype(BF)
    dh1 = (da * h3 * sig * (1.0 + h1 * (1.0 - sig))).astype(BF)
    dh = jnp.concatenate([dh1, dh3], axis=1)
    dx = lax.dot_general(dh, w13, NT, preferred_element_type=F32).astype(BF)
    dxr_ref[0] = dx.reshape(blocks, capacity, width)
    for b in range(blocks):
        col = dg[b * capacity:(b + 1) * capacity]
        dg_ref[0, pl.ds(m * blocks + b, 1), :] = jnp.sum(jnp.where(pos_rows[b] == place, col, 0.0), axis=0, keepdims=True)
    g13 = lax.dot_general(x, dh, TN, preferred_element_type=F32)
    g2 = lax.dot_general(act, g, TN, preferred_element_type=F32)

    @pl.when(m == 0)
    def _():
        acc13[...] = g13
        acc2[...] = g2

    @pl.when(m > 0)
    def _():
        acc13[...] += g13
        acc2[...] += g2

    @pl.when(m == pl.num_programs(1) - 1)
    def _():
        for z in range(4):
            cols = slice(z * LANES, z * LANES + LANES)
            for c in range(4):
                gw_ref[z, c // 2, 0, LANES * (c % 2):LANES * (c % 2) + LANES] = acc13[cols, c * LANES:c * LANES + LANES]
            gw_ref[z, 2, 0] = acc2[:, cols]


def expert_pass(first, count, pos, gate, rows, w_all):
    blocks = 4
    pairs, capacity, width = rows.shape[2:]
    tok = pos.shape[2]

    def row_spec(kind):
        return pl.BlockSpec((1, 1, blocks, capacity, width), lambda e, m: (kind, e + first, m, 0, 0))

    weights = w_all.shape[3:]
    fold = (4, 3, 1) + weights
    return pl.pallas_call(
        functools.partial(expert_kernel, first),
        grid=(count, pairs // blocks),
        out_shape=(jax.ShapeDtypeStruct((count, pairs, capacity, width), BF), jax.ShapeDtypeStruct((count, pairs, tok), F32), jax.ShapeDtypeStruct((4, 3, count) + weights, F32)),
        in_specs=[VM, VM, row_spec(0), row_spec(1), pl.BlockSpec(fold, lambda e, m: (0, 0, e + first, 0, 0))],
        out_specs=(pl.BlockSpec((1, blocks, capacity, width), lambda e, m: (e, m, 0, 0)), pl.BlockSpec((1, pairs, tok), lambda e, m: (e, 0, 0)), pl.BlockSpec(fold, lambda e, m: (0, 0, e, 0, 0))),
        scratch_shapes=[pltpu.VMEM((width, width), F32), pltpu.VMEM((weights[0], width), F32)],
        name='expert_pass',
        compiler_params=params(),
        cost_estimate=cost(6 * count, 10 * count),
    )(pos, gate, rows, rows, w_all)


def reduce_kernel(groups, *refs):
    post_ref, ids_ref = refs[:2]
    rows, dgs = refs[2:2 + groups], refs[2 + groups:2 + 2 * groups]
    dx_ref, dgate_ref, hot, near, far, far_dg, q_ref, g_ref, in_x, in_y, last_x, last_y, g_in, g_last, s_h, s_f, r_f, s_d, r_d, s_x, r_x, s_y, r_y, s_2x, r_2x, s_2y, r_2y, s_g, r_g = refs[2 + 2 * groups:]
    at = Place()
    capacity, width = near.shape[2:]
    tok = post_ref.shape[0]
    half = tok // 2
    upper = pl.ds(0, half)
    lower = pl.ds(half, half)
    swap, swap_dg, hop_x, hop_y, hop_2x, hop_2y, hop_g = (s_f, r_f), (s_d, r_d), (s_x, r_x), (s_y, r_y), (s_2x, r_2x), (s_2y, r_2y), (s_g, r_g)
    firsts = [sum(ref.shape[0] for ref in rows[:n]) for n in range(groups)]

    def span(n):
        return pl.ds(firsts[n], rows[n].shape[0])

    def pair_of(t):
        p, mb = lax.div(t, 2), lax.rem(t, 2)
        return (at.chip + (1 - lax.div(p, 2)) * at.to_x + (1 - lax.rem(p, 2)) * at.to_y) * 2 + mb

    def loads(t):
        b = lax.rem(t, 2)
        return [pltpu.make_async_copy(rows[n].at[:, at.core * 8 + pair_of(t)], near.at[b, span(n)], s_h.at[b, n]) for n in range(groups)]

    def swaps(t):
        return [rcopy(rows[n].at[:, at.other * 8 + pair_of(t)], far.at[t, span(n)], swap, (n, t), at.dev_c) for n in range(groups)]

    def swaps_dg():
        return [rcopy(dgs[n].at[:, pl.ds(pl.multiple_of(at.other * 8, 8), 8)], far_dg.at[span(n)], swap_dg, n, at.dev_c) for n in range(groups)]

    def send(src, dst, sems, i, dev):
        rcopy(src, dst, sems, i, dev).start()

    def sent(src, dst, sems, i, dev):
        rcopy(src, dst, sems, i, dev).wait_send()

    def first_hops(p, mb):
        hops = []
        if p < 2:
            hops.append((q_ref.at[p, mb, upper], in_x.at[mb, 1 - p], hop_x, 2 * mb + 1 - p, at.dev_x))
        if p % 2 == 0:
            hops.append((q_ref.at[p, mb, lower], in_y.at[mb, 1 - p // 2], hop_y, 2 * mb + 1 - p // 2, at.dev_y))
        return hops

    def gate_hop(p):
        return (g_ref.at[p], g_in.at[1 - p], hop_g, 1 - p, at.dev_x)

    for copy in loads(0):
        copy.start()
    at.greet()

    @pl.loop(0, 8)
    def _(t):
        for copy in swaps(t):
            copy.start()

        @pl.when(t == 0)
        def _():
            for copy in swaps_dg():
                copy.start()

    lane = iota((tok, LANES), 1)
    tiles = 2 * EXP * capacity // LANES

    @pl.loop(0, 8)
    def _(t):
        p, mb = lax.div(t, 2), lax.rem(t, 2)
        i = pair_of(t)

        @pl.when(t < 7)
        def _():
            for copy in loads(t + 1):
                copy.start()

        post = pltpu.roll(post_ref[...], lax.rem(LANES - i * 2 * EXP, LANES), 1)
        for k in range(tiles):
            col = k * LANES
            lo = col // capacity
            sel = post[:, lo:lo + 1] == lane + (col - lo * capacity)
            for e in range(lo + 1, (col + LANES - 1) // capacity + 1):
                sel = jnp.logical_or(sel, post[:, e:e + 1] == lane + (col - e * capacity))
            hot[:, col:col + LANES] = hot_bf(sel)
        for copy in loads(t):
            copy.wait()
        for copy in swaps(t):
            copy.wait_recv()

        @pl.when(t == 0)
        def _():
            for copy in swaps_dg():
                copy.wait_recv()

        rows_near = near[mb].reshape(EXP * capacity, width)
        rows_far = far[t].reshape(EXP * capacity, width)
        q_ref[p, mb] = dot(hot[...], jnp.concatenate([rows_near, rows_far], axis=0))
        ids = ids_ref[i]
        total = jnp.zeros(ids.shape, F32)
        for n in range(groups):
            for c in range(rows[n].shape[0]):
                e = firsts[n] + c
                mine = dgs[n][c, pl.ds(at.core * 8 + i, 1), :]
                total = jnp.where(ids == (at.me * EXP + e).astype(F32), mine, total)
                total = jnp.where(ids == (at.partner * EXP + e).astype(F32), far_dg[e, pl.ds(i, 1), :], total)
        g_ref[p, mb] = total
        for c in range(3):

            @pl.when(p == c)
            def _():
                for hop in first_hops(c, mb):
                    send(*hop)

        for c in range(2):

            @pl.when(t == 2 * c + 1)
            def _():
                send(*gate_hop(c))

    arrive(g_in.at[1], hop_g, 1, at.dev_x)
    g_in[1] += g_ref[2]
    gate_last = (g_in.at[1], g_last, hop_g, 2, at.dev_y)
    send(*gate_last)

    def last_hops(mb):
        return ((in_x.at[mb, 1], last_y.at[mb], hop_2y, mb, at.dev_y), (in_y.at[mb, 1], last_x.at[mb], hop_2x, mb, at.dev_x))

    for mb in range(2):
        hops = last_hops(mb)
        arrive(in_x.at[mb, 1], hop_x, 2 * mb + 1, at.dev_x)
        in_x[mb, 1] += q_ref[2, mb, upper]
        send(*hops[0])
        arrive(in_y.at[mb, 1], hop_y, 2 * mb + 1, at.dev_y)
        in_y[mb, 1] += q_ref[1, mb, lower]
        send(*hops[1])
    arrive(g_in.at[0], hop_g, 0, at.dev_x)
    arrive(g_last, hop_g, 2, at.dev_y)
    dgate_ref[...] = g_ref[3] + g_in[0] + g_last[...]
    for mb in range(2):
        arrive(in_x.at[mb, 0], hop_x, 2 * mb, at.dev_x)
        arrive(in_y.at[mb, 0], hop_y, 2 * mb, at.dev_y)
        q_ref[3, mb, upper] += in_x[mb, 0]
        q_ref[3, mb, lower] += in_y[mb, 0]
    for mb in range(2):
        arrive(last_y.at[mb], hop_2y, mb, at.dev_y)
        dx_ref[mb, upper] = (q_ref[3, mb, upper] + last_y[mb]).astype(BF)
        arrive(last_x.at[mb], hop_2x, mb, at.dev_x)
        dx_ref[mb, lower] = (q_ref[3, mb, lower] + last_x[mb]).astype(BF)
    for mb in range(2):
        sent(*gate_hop(mb))
        for c in range(3):
            for hop in first_hops(c, mb):
                sent(*hop)
        for hop in last_hops(mb):
            sent(*hop)
    sent(*gate_last)
    for copy in swaps_dg():
        copy.wait_send()

    @pl.loop(0, 8)
    def _(t):
        for copy in swaps(t):
            copy.wait_send()


def reduce_chips(post, ids, rows, dgs):
    groups = len(rows)
    capacity, width = rows[0].shape[2:]
    tok = post.shape[0]
    top_k = ids.shape[1]
    half = tok // 2
    dma = pltpu.SemaphoreType.DMA
    vm = pltpu.VMEM
    return pl.pallas_call(
        functools.partial(reduce_kernel, groups),
        out_shape=(jax.ShapeDtypeStruct((2, tok, width), BF), jax.ShapeDtypeStruct((2, top_k, tok), F32)),
        in_specs=[VM, VM] + [ANY] * groups + [VM] * groups,
        out_specs=(VM, VM),
        scratch_shapes=[vm((tok, 2 * EXP * capacity), BF), vm((2, EXP, capacity, width), BF), vm((8, EXP, capacity, width), BF), vm((EXP, 8, tok), F32), vm((4, 2, tok, width), F32), vm((4, 2, top_k, tok), F32)]
        + [vm((2, 2, half, width), F32)] * 2 + [vm((2, half, width), F32)] * 2 + [vm((2, 2, top_k, tok), F32), vm((2, top_k, tok), F32), dma((2, groups))]
        + [dma((groups, 8))] * 2 + [dma((groups,))] * 2 + [dma((4,))] * 4 + [dma((2,))] * 4 + [dma((3,))] * 2,
        name='reduce_chips',
        compiler_params=params(2),
        cost_estimate=cost(100, 40),
    )(post, ids, *rows, *dgs)


def solution(mesh):
    ep_size = mesh.shape['ep']
    tok_spec = P(None, ('fsdp', 'ep'), None)
    spec_edf = P('ep', 'fsdp', None)
    spec_efd = P('ep', None, 'fsdp')

    def fold(w):
        return jnp.concatenate([w[:, :, :LANES], w[:, :, LANES:]], axis=1)

    def unfold(g):
        return jnp.concatenate([g[:, :LANES], g[:, LANES:]], axis=2)

    def local_step(x_in, dy_out, expert_idx, gate_prob, w_one, w_two, w_three):
        micro, tok, width = x_in.shape
        top_k = expert_idx.shape[2]
        local_experts = w_one.shape[0]
        capacity = capacity_of(tok, top_k, local_experts * ep_size)
        w_mine = jnp.concatenate([fold(w_one), fold(w_three), w_two], axis=0)
        w_all = lax.all_gather(w_mine, 'fsdp', axis=0, tiled=False)
        w_all = w_all.reshape((w_all.shape[0], 3, local_experts) + w_two.shape[1:])
        meta = jnp.stack([jnp.transpose(expert_idx, (0, 2, 1)).astype(F32), jnp.transpose(gate_prob, (0, 2, 1))])
        rows, pos, gate, post, ids = gather_rows(x_in, dy_out, meta, capacity)
        dx_rows, dgs, grads = [], [], []
        for count in GROUPS:
            first = sum(r.shape[0] for r in dx_rows)
            r, d, g = expert_pass(first, count, pos, gate, rows, w_all)
            dx_rows.append(r)
            dgs.append(d)
            grads.append(lax.psum_scatter(g, 'fsdp', scatter_dimension=0, tiled=False))
        dx, dgate = reduce_chips(post, ids, dx_rows, dgs)
        grad = jnp.concatenate(grads, axis=1)
        return dx, jnp.transpose(dgate, (0, 2, 1)), unfold(grad[0]), grad[2], unfold(grad[1])

    return jax.shard_map(local_step, mesh=mesh, in_specs=(tok_spec, tok_spec, tok_spec, tok_spec, spec_edf, spec_efd, spec_edf), out_specs=(tok_spec, tok_spec, spec_edf, spec_efd, spec_edf), check_vma=False)
```

time: 1390 us -> 456 us (0.33)
  local copies, waits for them, and re-layouts: 662 us -> 4.54 us
  Pallas kernels: 0 us -> 421 us
  waiting for transfers between devices: 286 us -> 9.12 us
  matrix products: 224 us -> 0 us
  other arithmetic: 139 us -> 7.11 us
  starting transfers between devices: 49.3 us -> 0.34 us
    gather x10 -> x0, local copies, waits for them, and re-layouts: 450 us -> none  [the longest x2 114 us: local_step(): jnp.concatenate([gate_prob[mb_index].reshape(n_choice), zero_val])[holder]]
    pallas_call x0 -> x5, Pallas kernels: none -> 421 us  [the longest x1 181 us: gather_rows(): pl.pallas_call(functools.partial(gather_rows_kernel, capacity), out_shape...]
    all_to_all x10 -> x0, waiting for transfers between devices: 284 us -> none  [the longest x6 230 us: to_experts(): arrived = lax.all_to_all(send_buf, 'ep', 0, 2, tiled=True)]
    dot_general x18 -> x0, matrix products: 224 us -> none  [the longest x2 35.3 us: expert_pass(): jnp.einsum('erd,edf->erf', x_rows, w_three, preferred_element_type=jnp.fl...]
    another operation x8 -> x2, other arithmetic: 71.9 us -> 0.67 us  [local_step(): jnp.stack([jnp.transpose(expert_idx, (0, 2, 1)).astype(F32), jnp.transpos...]
    scatter x2 -> x0, local copies, waits for them, and re-layouts: 60.9 us -> none  [route_tables(): holder = holder.at[choice_slot].set(jnp.arange(n_choice, dtype=jnp.int32))]
    all_to_all x10 -> x0, starting transfers between devices: 48.3 us -> none  [the longest x6 30.2 us: to_experts(): arrived = lax.all_to_all(send_buf, 'ep', 0, 2, tiled=True)]
    convert_element_type x2 -> x0, local copies, waits for them, and re-layouts: 43.9 us -> none  [expert_pass(): g_rows = (gate_rows[:, :, None] * dy_rows).astype(jnp.bfloat16)]
  transfers between devices with their start and end apart: 16 -> 4, of which waited for: 5 -> 1; matrix products, arithmetic and copies ran while one was open for 58% -> 0% of each run, Pallas kernels for 0% -> 89%
where the time goes in v1:
time: 456 us
  Pallas kernels  421 us (92%)
  between operations  13.9 us (3%)
  waiting for transfers between devices  9.12 us (2%)
  other arithmetic  7.11 us (2%)
    pallas_call x1, Pallas kernels, gather_rows(): pl.pallas_call(functools.partial(gather_rows_kernel, capacity), out_shape...  181 us
    pallas_call x1, Pallas kernels, reduce_chips(): pl.pallas_call(functools.partial(reduce_kernel, groups), out_shape=(jax.S...  151 us
    pallas_call x3, Pallas kernels, expert_pass(): pl.pallas_call(functools.partial(expert_kernel, first), grid=(count, pair...  89.3 us
  transfers between devices with their start and end apart: 4, of which 1 were waited for; matrix products, arithmetic and copies ran while one was open for 0% of the time, Pallas kernels for 89%

profile of v1, /device:TPU:0, one launch (start us, length us, event | category | flops | bytes accessed | tf_op | source)
XLA Modules:
  0.0 456.1 jit_solution(13812769210085111024)
XLA Ops:
  7.2 0.0 copy-start.1
  7.2 0.0 copy-start.3
  7.2 0.0 all-gather.3.cloned.1.call-start
  7.2 1.3 fusion.2
  8.5 2.3 pad_maximum_fusion.1
  10.8 0.0 all-gather.3.cloned.1.call-update
  10.8 0.0 reduce-scatter.4.cloned.1.call-start
  10.9 0.0 copy-done.1
  10.9 0.0 copy-done.3
  10.9 0.7 pad_maximum_fusion.4.meta_ref
  11.6 180.9 %gather_rows.1 = (bf16[2,8,16,160,512]{4,3,2,1,0:T(8,128)(2,1)}, f32[16,8,1024]{2,1,0:T(8,128)}, f32[16,8,1024]{2,1,0:T(8,128)}, f32[1024,128]{1,0:T(8,128)}, f32[8,8,1024]{2,1,0:T(8,128)}) custom-call(bf16[2,1024,512]{2,1,0:T(8,128)(2,1)} %x_ref.1, bf16[2,1024,512]{2,1,0:T(8,128)(2,1)} %dy_ref.1, f32[2,2,8,1024]{3,2,1,0:T(8,128)} %pad_maximum_fusion.4.meta_ref), custom_call_target="tpu_custom_call" | custom-call | flops 99999997952 | bytes 80000000 | tf_op jit(solution)/shard_map/gather_rows/pallas_call | solution.py:263
  192.5 0.0 all-gather.3.cloned.1.call-done
  192.6 13.0 %expert_pass.3 = (bf16[1,16,160,512]{3,2,1,0:T(8,128)(2,1)}, f32[1,16,1024]{2,1,0:T(8,128)}, f32[4,3,1,256,128]{4,3,2,1,0:T(8,128)}) custom-call(f32[16,8,1024]{2,1,0:T(8,128)} %get-tuple-element.23.pos_ref, f32[16,8,1024]{2,1,0:T(8,128)} %get-tuple-element.24.gate_ref, bf16[2,8,16,160,512]{4,3,2,1,0:T(8,128)(2,1)} %get-tuple-element.25.xr_ref.dyr_ref, ...), custom_call_target="tpu_custom_call" | custom-call | flops 6000000000 | bytes 10000000 | tf_op jit(solution)/shard_map/expert_pass/pallas_call | solution.py:340
  205.6 0.0 reduce-scatter.4.cloned.1.call-update
  205.6 0.0 reduce-scatter.6.cloned.1.call-start
  205.7 33.2 %expert_pass.4 = (bf16[3,16,160,512]{3,2,1,0:T(8,128)(2,1)}, f32[3,16,1024]{2,1,0:T(8,128)}, f32[4,3,3,256,128]{4,3,2,1,0:T(8,128)}) custom-call(f32[16,8,1024]{2,1,0:T(8,128)} %get-tuple-element.23.pos_ref, f32[16,8,1024]{2,1,0:T(8,128)} %get-tuple-element.24.gate_ref, bf16[2,8,16,160,512]{4,3,2,1,0:T(8,128)(2,1)} %get-tuple-element.25.xr_ref.dyr_ref, ...), custom_call_target="tpu_custom_call" | custom-call | flops 17999998976 | bytes 30000000 | tf_op jit(solution)/shard_map/expert_pass/pallas_call | solution.py:340
  238.9 0.0 reduce-scatter.6.cloned.1.call-update
  238.9 0.2 reduce-scatter.8.cloned.1.call-start
  239.1 43.1 %expert_pass.5 = (bf16[4,16,160,512]{3,2,1,0:T(8,128)(2,1)}, f32[4,16,1024]{2,1,0:T(8,128)}, f32[4,3,4,256,128]{4,3,2,1,0:T(8,128)}) custom-call(f32[16,8,1024]{2,1,0:T(8,128)} %get-tuple-element.23.pos_ref, f32[16,8,1024]{2,1,0:T(8,128)} %get-tuple-element.24.gate_ref, bf16[2,8,16,160,512]{4,3,2,1,0:T(8,128)(2,1)} %get-tuple-element.25.xr_ref.dyr_ref, ...), custom_call_target="tpu_custom_call" | custom-call | flops 24000000000 | bytes 40000000 | tf_op jit(solution)/shard_map/expert_pass/pallas_call | solution.py:340
  282.2 0.0 reduce-scatter.8.cloned.1.call-update
  282.2 150.8 %reduce_chips.1 = (bf16[2,1024,512]{2,1,0:T(8,128)(2,1)}, f32[2,8,1024]{2,1,0:T(8,128)}) custom-call(f32[1024,128]{1,0:T(8,128)} %get-tuple-element.21.refs_0_, f32[8,8,1024]{2,1,0:T(8,128)} %get-tuple-element.22.refs_1_, bf16[1,16,160,512]{3,2,1,0:T(8,128)(2,1)} %get-tuple-element.26.refs_2_, bf16[3,16,160,512]{3,2,1,0:T(8,128)(2,1)} %get-tuple-element.27.refs_3_, ...), custom_call_target="tpu_custom_call" | custom-call | flops 99999997952 | bytes 40000000 | tf_op jit(solution)/shard_map/reduce_chips/pallas_call | solution.py:524
  433.1 0.0 reduce-scatter.4.cloned.1.call-done
  433.1 0.0 reduce-scatter.6.cloned.1.call-done
  433.1 9.0 %reduce-scatter.8.cloned.1.call-done = f32[1,3,4,256,128]{4,3,2,1,0:T(8,128)} async-done(((f32[4,3,4,256,128]{4,3,2,1,0:T(8,128)}), f32[1,3,4,256,128]{4,3,2,1,0:T(8,128)}) %reduce-scatter.8.cloned.1.call-update) | async-done | bytes 1572880 | tf_op jit(solution)/shard_map/reduce_scatter | solution.py:566
  442.1 2.0 pad_maximum_fusion
  444.1 1.2 slice_bitcast_fusion
  445.3 0.1 fusion
  445.4 0.0 copy-start
  445.4 0.1 fusion.1
  445.5 1.0 pad_maximum_fusion.3
  446.5 0.0 copy-start.2
  446.5 1.0 pad_maximum_fusion.2
  447.6 0.0 copy-done
  447.6 1.3 copy.16
  448.9 0.0 copy-done.2
  448.9 0.6 copy.17
  (1 shorter events, 0.0 us)
Async XLA Ops:
  7.2 3.7 copy-start.1
  7.2 3.7 copy-start.3
  7.2 185.4 %all-gather.3.cloned.1.call-start = ((), (), s32[]{:S(2)}) async-start(), calls=%async_computation.6 | async-start | bytes 7864320 | tf_op jit(solution)/shard_map/all_gather | solution.py:556
  10.8 422.2 %reduce-scatter.4.cloned.1.call-start = ((), (), s32[]{:S(2)}) async-start(), calls=%async_computation.3 | async-start | bytes 1966080 | tf_op jit(solution)/shard_map/reduce_scatter | solution.py:566
  205.6 227.5 %reduce-scatter.6.cloned.1.call-start = ((), (), s32[]{:S(2)}) async-start(), calls=%async_computation.4 | async-start | bytes 5898240 | tf_op jit(solution)/shard_map/reduce_scatter | solution.py:566
  238.9 203.2 %reduce-scatter.8.cloned.1.call-start = ((), (), s32[]{:S(2)}) async-start(), calls=%async_computation.5 | async-start | bytes 7864320 | tf_op jit(solution)/shard_map/reduce_scatter | solution.py:566
  445.4 2.2 copy-start
  446.5 2.4 copy-start.2
Sparse Core Ops, SparseCore 0:
  11.0 117.6 all-gather.2
  205.8 36.8 reduce-scatter.3
  244.9 83.7 reduce-scatter.5
  330.9 111.1 reduce-scatter.7

commit v2 on v1

--- a/solution.py
+++ b/solution.py
@@ -63,11 +63,11 @@
         self.chip_d = self.chip_x + self.to_y
         self.dev_x = (z, 2 * self.chip_x + self.core)
         self.dev_y = (z, 2 * self.chip_y + self.core)
+        self.dev_d = (z, 2 * self.chip_d + self.core)
         self.dev_c = (z, self.partner)
 
-    def greet(self):
+    def greet(self, *devices):
         barrier = pltpu.get_barrier_semaphore()
-        devices = (self.dev_x, self.dev_y, self.dev_c)
         for dev in devices:
             pl.semaphore_signal(barrier, inc=1, device_id=dev, device_id_type=MESH)
         pl.semaphore_wait(barrier, len(devices))
@@ -103,8 +103,6 @@
         return tg.at[(k - 1) % 2, slot, (k - 1) // 2]
 
     def part(k, slot, h):
-        if k == 0:
-            return mg.at[slot, h]
         return block(k, slot).at[pl.ds(h * half, half)]
 
     slot = slot_of(at.core, at.chip)
@@ -124,7 +122,13 @@
         return ((part(k, slot_d, 0), part(k, slot_d, 0), fwd_a, k, at.dev_c), (part(k, slot_d, 1), part(k, slot_d, 1), fwd_b, k, at.dev_c))
 
     def own_hops(k):
-        return tuple((own(k), block(k, slot), sems, k, dev) for sems, dev in ((by_x, at.dev_x), (by_y, at.dev_y), (by_c, at.dev_c)))
+        return tuple((own(k), block(k, slot), sems, k, dev) for sems, dev in ((by_c, at.dev_c), (by_x, at.dev_x), (by_y, at.dev_y)))
+
+    def meta_hops():
+        return tuple((meta_ref, mg.at[slot], sems, 0, dev) for sems, dev in ((relay_x, at.dev_d), (by_x, at.dev_x), (by_y, at.dev_y), (by_c, at.dev_c)))
+
+    def meta_shares():
+        return tuple((mg.at[src], mg.at[src], sems, 0, at.dev_c) for src, sems in ((slot_x, fwd_x), (slot_y, fwd_y), (slot_d, fwd_a)))
 
     def send(hops):
         for hop in hops:
@@ -152,18 +156,21 @@
     local = [pltpu.make_async_copy(own(k), block(k, slot), s_l.at[k]) for k in chunks]
     for copy in local:
         copy.start()
-    at.greet()
-    for k in chunks:
-        send(own_hops(k)[:2])
-    for k in chunks:
-        send(own_hops(k)[2:])
+    at.greet(at.dev_x, at.dev_y, at.dev_d, at.dev_c)
+    send(meta_hops())
+    for k in chunks[1:]:
+        send(own_hops(k))
 
     tri[...] = hot_bf(iota((tok, tok), 0) < iota((tok, tok), 1))
     for copy in local:
         copy.wait()
-    arrive(block(0, slot_of(at.other, at.chip)), by_c, 0, at.dev_c)
-    pass_on(0)
-    pass_on_corner(0)
+    arrive(mg.at[slot_of(at.other, at.chip)], by_c, 0, at.dev_c)
+    shared = meta_shares()
+    for n, (src, sems, dev) in enumerate(((slot_x, by_x, at.dev_x), (slot_y, by_y, at.dev_y), (slot_d, relay_x, at.dev_d))):
+        arrive(mg.at[src], sems, 0, dev)
+        send(shared[n:n + 1])
+    for chip, sems in ((at.chip_x, fwd_x), (at.chip_y, fwd_y), (at.chip_d, fwd_a)):
+        arrive(mg.at[slot_of(at.other, chip)], sems, 0, at.dev_c)
     sub = iota((EXP, tok), 0)
 
     def hot_of(src, mb, device):
@@ -250,7 +257,9 @@
 
     for b in range(2):
         stored(b, 0, b).wait()
-    for k in chunks:
+    for hop in meta_hops() + meta_shares():
+        rcopy(*hop).wait_send()
+    for k in chunks[1:]:
         for hop in own_hops(k) + side_hops(k) + corner_hops(k):
             rcopy(*hop).wait_send()
 
@@ -328,7 +337,7 @@
 
 
 def expert_pass(first, count, pos, gate, rows, w_all):
-    blocks = 4
+    blocks = 8
     pairs, capacity, width = rows.shape[2:]
     tok = pos.shape[2]
 
@@ -399,7 +408,7 @@
 
     for copy in loads(0):
         copy.start()
-    at.greet()
+    at.greet(at.dev_x, at.dev_y, at.dev_c)
 
     @pl.loop(0, 8)
     def _(t):

time: 456 us -> 428 us (0.939)
  Pallas kernels: 421 us -> 390 us
    pallas_call x1, Pallas kernels: 181 us -> 153 us  [gather_rows(): pl.pallas_call(functools.partial(gather_rows_kernel, capacity), out_shape...]
  transfers between devices with their start and end apart: 4 -> 4, of which waited for: 1 -> 1; matrix products, arithmetic and copies ran while one was open for 0% -> 0% of each run, Pallas kernels for 89% -> 88%
where the time goes in v2:
time: 428 us
  Pallas kernels  390 us (91%)
  between operations  13.9 us (3%)
  waiting for transfers between devices  12.6 us (3%)
  other arithmetic  7.11 us (2%)
  local copies, waits for them, and re-layouts  4.54 us (1%)
    pallas_call x1, Pallas kernels, gather_rows(): pl.pallas_call(functools.partial(gather_rows_kernel, capacity), out_shape...  153 us
    pallas_call x1, Pallas kernels, reduce_chips(): pl.pallas_call(functools.partial(reduce_kernel, groups), out_shape=(jax.S...  151 us
    pallas_call x3, Pallas kernels, expert_pass(): pl.pallas_call(functools.partial(expert_kernel, first), grid=(count, pair...  85.9 us
    reduce_scatter x3, waiting for transfers between devices, local_step(): grads.append(lax.psum_scatter(g, 'fsdp', scatter_dimension=0, tiled=False))  12.5 us
  transfers between devices with their start and end apart: 4, of which 1 were waited for; matrix products, arithmetic and copies ran while one was open for 0% of the time, Pallas kernels for 88%

profile of v2, /device:TPU:0, one launch (start us, length us, event | category | flops | bytes accessed | tf_op | source)
XLA Modules:
  0.0 428.2 jit_solution(2809697844444575912)
XLA Ops:
  7.2 0.0 copy-start.1
  7.2 0.0 copy-start.3
  7.2 0.0 all-gather.3.cloned.1.call-start
  7.2 1.3 fusion.2
  8.5 2.3 pad_maximum_fusion.1
  10.8 0.0 all-gather.3.cloned.1.call-update
  10.8 0.0 reduce-scatter.4.cloned.1.call-start
  10.9 0.0 copy-done.1
  10.9 0.0 copy-done.3
  10.9 0.7 pad_maximum_fusion.4.meta_ref
  11.6 153.3 %gather_rows.1 = (bf16[2,8,16,160,512]{4,3,2,1,0:T(8,128)(2,1)}, f32[16,8,1024]{2,1,0:T(8,128)}, f32[16,8,1024]{2,1,0:T(8,128)}, f32[1024,128]{1,0:T(8,128)}, f32[8,8,1024]{2,1,0:T(8,128)}) custom-call(bf16[2,1024,512]{2,1,0:T(8,128)(2,1)} %x_ref.1, bf16[2,1024,512]{2,1,0:T(8,128)(2,1)} %dy_ref.1, f32[2,2,8,1024]{3,2,1,0:T(8,128)} %pad_maximum_fusion.4.meta_ref), custom_call_target="tpu_custom_call" | custom-call | flops 99999997952 | bytes 80000000 | tf_op jit(solution)/shard_map/gather_rows/pallas_call | solution.py:272
  164.9 0.0 all-gather.3.cloned.1.call-done
  165.0 13.1 %expert_pass.3 = (bf16[1,16,160,512]{3,2,1,0:T(8,128)(2,1)}, f32[1,16,1024]{2,1,0:T(8,128)}, f32[4,3,1,256,128]{4,3,2,1,0:T(8,128)}) custom-call(f32[16,8,1024]{2,1,0:T(8,128)} %get-tuple-element.23.pos_ref, f32[16,8,1024]{2,1,0:T(8,128)} %get-tuple-element.24.gate_ref, bf16[2,8,16,160,512]{4,3,2,1,0:T(8,128)(2,1)} %get-tuple-element.25.xr_ref.dyr_ref, ...), custom_call_target="tpu_custom_call" | custom-call | flops 6000000000 | bytes 10000000 | tf_op jit(solution)/shard_map/expert_pass/pallas_call | solution.py:349
  178.0 0.0 reduce-scatter.4.cloned.1.call-update
  178.1 0.0 reduce-scatter.6.cloned.1.call-start
  178.1 31.8 %expert_pass.4 = (bf16[3,16,160,512]{3,2,1,0:T(8,128)(2,1)}, f32[3,16,1024]{2,1,0:T(8,128)}, f32[4,3,3,256,128]{4,3,2,1,0:T(8,128)}) custom-call(f32[16,8,1024]{2,1,0:T(8,128)} %get-tuple-element.23.pos_ref, f32[16,8,1024]{2,1,0:T(8,128)} %get-tuple-element.24.gate_ref, bf16[2,8,16,160,512]{4,3,2,1,0:T(8,128)(2,1)} %get-tuple-element.25.xr_ref.dyr_ref, ...), custom_call_target="tpu_custom_call" | custom-call | flops 17999998976 | bytes 30000000 | tf_op jit(solution)/shard_map/expert_pass/pallas_call | solution.py:349
  209.9 0.0 reduce-scatter.6.cloned.1.call-update
  209.9 0.2 reduce-scatter.8.cloned.1.call-start
  210.1 41.1 %expert_pass.5 = (bf16[4,16,160,512]{3,2,1,0:T(8,128)(2,1)}, f32[4,16,1024]{2,1,0:T(8,128)}, f32[4,3,4,256,128]{4,3,2,1,0:T(8,128)}) custom-call(f32[16,8,1024]{2,1,0:T(8,128)} %get-tuple-element.23.pos_ref, f32[16,8,1024]{2,1,0:T(8,128)} %get-tuple-element.24.gate_ref, bf16[2,8,16,160,512]{4,3,2,1,0:T(8,128)(2,1)} %get-tuple-element.25.xr_ref.dyr_ref, ...), custom_call_target="tpu_custom_call" | custom-call | flops 24000000000 | bytes 40000000 | tf_op jit(solution)/shard_map/expert_pass/pallas_call | solution.py:349
  251.2 0.0 reduce-scatter.8.cloned.1.call-update
  251.2 150.6 %reduce_chips.1 = (bf16[2,1024,512]{2,1,0:T(8,128)(2,1)}, f32[2,8,1024]{2,1,0:T(8,128)}) custom-call(f32[1024,128]{1,0:T(8,128)} %get-tuple-element.21.refs_0_, f32[8,8,1024]{2,1,0:T(8,128)} %get-tuple-element.22.refs_1_, bf16[1,16,160,512]{3,2,1,0:T(8,128)(2,1)} %get-tuple-element.26.refs_2_, bf16[3,16,160,512]{3,2,1,0:T(8,128)(2,1)} %get-tuple-element.27.refs_3_, ...), custom_call_target="tpu_custom_call" | custom-call | flops 99999997952 | bytes 40000000 | tf_op jit(solution)/shard_map/reduce_chips/pallas_call | solution.py:533
  401.8 0.0 reduce-scatter.4.cloned.1.call-done
  401.8 0.0 reduce-scatter.6.cloned.1.call-done
  401.9 12.4 %reduce-scatter.8.cloned.1.call-done = f32[1,3,4,256,128]{4,3,2,1,0:T(8,128)} async-done(((f32[4,3,4,256,128]{4,3,2,1,0:T(8,128)}), f32[1,3,4,256,128]{4,3,2,1,0:T(8,128)}) %reduce-scatter.8.cloned.1.call-update) | async-done | bytes 1572880 | tf_op jit(solution)/shard_map/reduce_scatter | solution.py:575
  414.3 2.0 pad_maximum_fusion
  416.3 1.2 slice_bitcast_fusion
  417.5 0.1 fusion
  417.6 0.0 copy-start
  417.6 0.1 fusion.1
  417.7 1.0 pad_maximum_fusion.3
  418.7 0.0 copy-start.2
  418.7 1.0 pad_maximum_fusion.2
  419.8 0.0 copy-done
  419.8 1.3 copy.16
  421.1 0.0 copy-done.2
  421.1 0.6 copy.17
  (1 shorter events, 0.0 us)
Async XLA Ops:
  7.2 3.7 copy-start.1
  7.2 3.7 copy-start.3
  7.2 157.8 %all-gather.3.cloned.1.call-start = ((), (), s32[]{:S(2)}) async-start(), calls=%async_computation.6 | async-start | bytes 7864320 | tf_op jit(solution)/shard_map/all_gather | solution.py:565
  10.8 391.0 %reduce-scatter.4.cloned.1.call-start = ((), (), s32[]{:S(2)}) async-start(), calls=%async_computation.3 | async-start | bytes 1966080 | tf_op jit(solution)/shard_map/reduce_scatter | solution.py:575
  178.1 223.8 %reduce-scatter.6.cloned.1.call-start = ((), (), s32[]{:S(2)}) async-start(), calls=%async_computation.4 | async-start | bytes 5898240 | tf_op jit(solution)/shard_map/reduce_scatter | solution.py:575
  209.9 204.4 %reduce-scatter.8.cloned.1.call-start = ((), (), s32[]{:S(2)}) async-start(), calls=%async_computation.5 | async-start | bytes 7864320 | tf_op jit(solution)/shard_map/reduce_scatter | solution.py:575
  417.6 2.2 copy-start
  418.7 2.4 copy-start.2
Sparse Core Ops, SparseCore 0:
  11.0 117.6 all-gather.2
  178.2 36.6 reduce-scatter.3
  217.1 83.7 reduce-scatter.5
  303.1 111.1 reduce-scatter.7

commit v3 on v2

--- a/solution.py
+++ b/solution.py
@@ -13,7 +13,7 @@
 ANY = pl.BlockSpec(memory_space=pl.ANY)
 VM = pl.BlockSpec(memory_space=pltpu.VMEM)
 VLIM = 62 * 1024 * 1024
-GROUPS = (1, 3, 4)
+GROUPS = (2, 6)
 DROPPED = -4096.0
 LANES = 128
 EXP = 8
@@ -281,7 +281,7 @@
     )(x_in, dy_out, meta)
 
 
-def expert_kernel(first, pos_ref, gate_ref, xr_ref, dyr_ref, wa_ref, dxr_ref, dg_ref, gw_ref, acc13, acc2):
+def expert_kernel(first, pos_ref, gate_ref, xr_ref, dyr_ref, w1_ref, w3_ref, w2_ref, dxr_ref, dg_ref, gw_ref, acc13, acc2):
     m = pl.program_id(1)
     e = pl.program_id(0) + first
     blocks, capacity, width = xr_ref.shape[2:]
@@ -289,10 +289,9 @@
     rows = blocks * capacity
     x = xr_ref[0, 0].reshape(rows, width)
     dy = dyr_ref[0, 0].reshape(rows, width)
-    folds = [wa_ref[:, c // 2, 0, LANES * (c % 2):LANES * (c % 2) + LANES].reshape(width, LANES) for c in range(4)]
-    w13 = jnp.concatenate(folds, axis=1)
-    w2 = jnp.concatenate([wa_ref[z, 2, 0] for z in range(4)], axis=1)
-    ff = w2.shape[0]
+    ff = w1_ref.shape[3]
+    w13 = jnp.concatenate([w1_ref[:, 0].reshape(width, ff), w3_ref[:, 0].reshape(width, ff)], axis=1)
+    w2 = jnp.concatenate([w2_ref[z, 0] for z in range(4)], axis=1)
     place = iota((capacity, tok), 0)
     pos_rows = [pos_ref[m * blocks + b, pl.ds(e, 1), :] for b in range(blocks)]
     q = jnp.concatenate([jnp.sum(jnp.where(pos_rows[b] == place, gate_ref[m * blocks + b, pl.ds(e, 1), :], 0.0), axis=1, keepdims=True) for b in range(blocks)], axis=0)
@@ -336,7 +335,7 @@
             gw_ref[z, 2, 0] = acc2[:, cols]
 
 
-def expert_pass(first, count, pos, gate, rows, w_all):
+def expert_pass(first, count, pos, gate, rows, w_one, w_three, w_two):
     blocks = 8
     pairs, capacity, width = rows.shape[2:]
     tok = pos.shape[2]
@@ -344,19 +343,22 @@
     def row_spec(kind):
         return pl.BlockSpec((1, 1, blocks, capacity, width), lambda e, m: (kind, e + first, m, 0, 0))
 
-    weights = w_all.shape[3:]
+    def w_spec(w):
+        return pl.BlockSpec((w.shape[0], 1) + w.shape[2:], lambda e, m: (0, e + first, 0, 0))
+
+    weights = w_two.shape[2:]
     fold = (4, 3, 1) + weights
     return pl.pallas_call(
         functools.partial(expert_kernel, first),
         grid=(count, pairs // blocks),
         out_shape=(jax.ShapeDtypeStruct((count, pairs, capacity, width), BF), jax.ShapeDtypeStruct((count, pairs, tok), F32), jax.ShapeDtypeStruct((4, 3, count) + weights, F32)),
-        in_specs=[VM, VM, row_spec(0), row_spec(1), pl.BlockSpec(fold, lambda e, m: (0, 0, e + first, 0, 0))],
+        in_specs=[VM, VM, row_spec(0), row_spec(1), w_spec(w_one), w_spec(w_three), w_spec(w_two)],
         out_specs=(pl.BlockSpec((1, blocks, capacity, width), lambda e, m: (e, m, 0, 0)), pl.BlockSpec((1, pairs, tok), lambda e, m: (e, 0, 0)), pl.BlockSpec(fold, lambda e, m: (0, 0, e, 0, 0))),
         scratch_shapes=[pltpu.VMEM((width, width), F32), pltpu.VMEM((weights[0], width), F32)],
         name='expert_pass',
         compiler_params=params(),
         cost_estimate=cost(6 * count, 10 * count),
-    )(pos, gate, rows, rows, w_all)
+    )(pos, gate, rows, rows, w_one, w_three, w_two)
 
 
 def reduce_kernel(groups, *refs):
@@ -550,26 +552,22 @@
     spec_edf = P('ep', 'fsdp', None)
     spec_efd = P('ep', None, 'fsdp')
 
-    def fold(w):
-        return jnp.concatenate([w[:, :, :LANES], w[:, :, LANES:]], axis=1)
-
     def unfold(g):
-        return jnp.concatenate([g[:, :LANES], g[:, LANES:]], axis=2)
+        halves = g.reshape(g.shape[0], -1, LANES, LANES)
+        return jnp.swapaxes(halves, 1, 2).reshape(g.shape[0], LANES, -1)
 
     def local_step(x_in, dy_out, expert_idx, gate_prob, w_one, w_two, w_three):
         micro, tok, width = x_in.shape
         top_k = expert_idx.shape[2]
         local_experts = w_one.shape[0]
         capacity = capacity_of(tok, top_k, local_experts * ep_size)
-        w_mine = jnp.concatenate([fold(w_one), fold(w_three), w_two], axis=0)
-        w_all = lax.all_gather(w_mine, 'fsdp', axis=0, tiled=False)
-        w_all = w_all.reshape((w_all.shape[0], 3, local_experts) + w_two.shape[1:])
+        w_all = [lax.all_gather(w, 'fsdp', axis=0, tiled=False) for w in (w_one, w_three, w_two)]
         meta = jnp.stack([jnp.transpose(expert_idx, (0, 2, 1)).astype(F32), jnp.transpose(gate_prob, (0, 2, 1))])
         rows, pos, gate, post, ids = gather_rows(x_in, dy_out, meta, capacity)
         dx_rows, dgs, grads = [], [], []
         for count in GROUPS:
             first = sum(r.shape[0] for r in dx_rows)
-            r, d, g = expert_pass(first, count, pos, gate, rows, w_all)
+            r, d, g = expert_pass(first, count, pos, gate, rows, *w_all)
             dx_rows.append(r)
             dgs.append(d)
             grads.append(lax.psum_scatter(g, 'fsdp', scatter_dimension=0, tiled=False))

time: 428 us -> 426 us (level)
    concatenate x3 -> x0, other arithmetic: 4.41 us -> none  [the longest x1 2.32 us: local_step(): w_mine = jnp.concatenate([fold(w_one), fold(w_three), w_two], axis=0)]
    pallas_call x3 -> x2, Pallas kernels: 85.9 us -> 82.6 us  [expert_pass(): pl.pallas_call(functools.partial(expert_kernel, first), grid=(count, pair...]
    reduce_scatter x3 -> x2, waiting for transfers between devices: 12.5 us -> 13.7 us  [local_step(): grads.append(lax.psum_scatter(g, 'fsdp', scatter_dimension=0, tiled=False))]
  transfers between devices with their start and end apart: 4 -> 5, of which waited for: 1 -> 1; matrix products, arithmetic and copies ran while one was open for 0% -> 1% of each run, Pallas kernels for 88% -> 85%
where the time goes in v3:
time: 426 us
  Pallas kernels  386 us (91%)
  waiting for transfers between devices  15.9 us (4%)
  between operations  13.8 us (3%)
  other arithmetic  5.37 us (1%)
  local copies, waits for them, and re-layouts  4.3 us (1%)
    pallas_call x1, Pallas kernels, gather_rows(): pl.pallas_call(functools.partial(gather_rows_kernel, capacity), out_shape...  153 us
    pallas_call x1, Pallas kernels, reduce_chips(): pl.pallas_call(functools.partial(reduce_kernel, groups), out_shape=(jax.S...  150 us
    pallas_call x2, Pallas kernels, expert_pass(): pl.pallas_call(functools.partial(expert_kernel, first), grid=(count, pair...  82.6 us
    reduce_scatter x2, waiting for transfers between devices, local_step(): grads.append(lax.psum_scatter(g, 'fsdp', scatter_dimension=0, tiled=False))  13.7 us
  transfers between devices with their start and end apart: 5, of which 1 were waited for; matrix products, arithmetic and copies ran while one was open for 1% of the time, Pallas kernels for 85%

profile of v3, /device:TPU:0, one launch (start us, length us, event | category | flops | bytes accessed | tf_op | source)
XLA Modules:
  0.0 425.9 jit_solution(4683503218702321509)
XLA Ops:
  7.2 0.0 all-gather.7.cloned.1.call-start
  7.2 0.7 all-gather.7.cloned.1.call-update
  7.9 0.0 all-gather.9.cloned.1.call-start
  7.9 0.7 all-gather.9.cloned.1.call-update
  8.7 0.0 all-gather.11.cloned.1.call-start
  8.7 0.7 all-gather.11.cloned.1.call-update
  9.4 0.0 reduce-scatter.3.cloned.1.call-start
  9.4 0.8 convert_bitcast_fusion
  10.3 1.5 pad_maximum_fusion.1.meta_ref
  11.8 153.3 %gather_rows.1 = (bf16[2,8,16,160,512]{4,3,2,1,0:T(8,128)(2,1)}, f32[16,8,1024]{2,1,0:T(8,128)}, f32[16,8,1024]{2,1,0:T(8,128)}, f32[1024,128]{1,0:T(8,128)}, f32[8,8,1024]{2,1,0:T(8,128)}) custom-call(bf16[2,1024,512]{2,1,0:T(8,128)(2,1)} %x_ref.1, bf16[2,1024,512]{2,1,0:T(8,128)(2,1)} %dy_ref.1, f32[2,2,8,1024]{3,2,1,0:T(8,128)} %pad_maximum_fusion.1.meta_ref), custom_call_target="tpu_custom_call" | custom-call | flops 99999997952 | bytes 80000000 | tf_op jit(solution)/shard_map/gather_rows/pallas_call | solution.py:272
  165.0 0.0 all-gather.7.cloned.1.call-done
  165.1 0.0 all-gather.9.cloned.1.call-done
  165.1 0.0 all-gather.11.cloned.1.call-done
  165.1 22.5 %expert_pass.2 = (bf16[2,16,160,512]{3,2,1,0:T(8,128)(2,1)}, f32[2,16,1024]{2,1,0:T(8,128)}, f32[4,3,2,256,128]{4,3,2,1,0:T(8,128)}) custom-call(f32[16,8,1024]{2,1,0:T(8,128)} %get-tuple-element.20.pos_ref, f32[16,8,1024]{2,1,0:T(8,128)} %get-tuple-element.21.gate_ref, bf16[2,8,16,160,512]{4,3,2,1,0:T(8,128)(2,1)} %get-tuple-element.22.xr_ref.dyr_ref, ...), custom_call_target="tpu_custom_call" | custom-call | flops 12000000000 | bytes 20000000 | tf_op jit(solution)/shard_map/expert_pass/pallas_call | solution.py:351
  187.6 0.0 reduce-scatter.3.cloned.1.call-update
  187.6 0.2 reduce-scatter.5.cloned.1.call-start
  187.9 60.1 %expert_pass.3 = (bf16[6,16,160,512]{3,2,1,0:T(8,128)(2,1)}, f32[6,16,1024]{2,1,0:T(8,128)}, f32[4,3,6,256,128]{4,3,2,1,0:T(8,128)}) custom-call(f32[16,8,1024]{2,1,0:T(8,128)} %get-tuple-element.20.pos_ref, f32[16,8,1024]{2,1,0:T(8,128)} %get-tuple-element.21.gate_ref, bf16[2,8,16,160,512]{4,3,2,1,0:T(8,128)(2,1)} %get-tuple-element.22.xr_ref.dyr_ref, ...), custom_call_target="tpu_custom_call" | custom-call | flops 35999997952 | bytes 60000000 | tf_op jit(solution)/shard_map/expert_pass/pallas_call | solution.py:351
  248.0 0.0 reduce-scatter.5.cloned.1.call-update
  248.0 150.3 %reduce_chips.1 = (bf16[2,1024,512]{2,1,0:T(8,128)(2,1)}, f32[2,8,1024]{2,1,0:T(8,128)}) custom-call(f32[1024,128]{1,0:T(8,128)} %get-tuple-element.18.refs_0_, f32[8,8,1024]{2,1,0:T(8,128)} %get-tuple-element.19.refs_1_, bf16[2,16,160,512]{3,2,1,0:T(8,128)(2,1)} %get-tuple-element.23.refs_2_, bf16[6,16,160,512]{3,2,1,0:T(8,128)(2,1)} %get-tuple-element.24.refs_3_, ...), custom_call_target="tpu_custom_call" | custom-call | flops 99999997952 | bytes 40000000 | tf_op jit(solution)/shard_map/reduce_chips/pallas_call | solution.py:535
  398.3 0.0 reduce-scatter.3.cloned.1.call-done
  398.4 13.7 %reduce-scatter.5.cloned.1.call-done = f32[1,3,6,256,128]{4,3,2,1,0:T(8,128)} async-done(((f32[4,3,6,256,128]{4,3,2,1,0:T(8,128)}), f32[1,3,6,256,128]{4,3,2,1,0:T(8,128)}) %reduce-scatter.5.cloned.1.call-update) | async-done | bytes 2359312 | tf_op jit(solution)/shard_map/reduce_scatter | solution.py:573
  412.1 3.0 pad_maximum_fusion
  415.1 0.0 copy-start
  415.1 1.5 copy_bitcast_fusion
  416.6 0.0 copy-start.1
  416.6 0.8 copy-done
  417.4 1.3 copy.22
  418.8 0.0 copy-done.1
  418.8 0.6 copy.23
Async XLA Ops:
  7.2 157.9 %all-gather.7.cloned.1.call-start = ((), (), s32[]{:S(2)}) async-start(), calls=%async_computation.4 | async-start | bytes 2621440 | tf_op jit(solution)/shard_map/all_gather | solution.py:564
  7.9 157.2 %all-gather.9.cloned.1.call-start = ((), (), s32[]{:S(2)}) async-start(), calls=%async_computation.5 | async-start | bytes 2621440 | tf_op jit(solution)/shard_map/all_gather | solution.py:564
  8.7 156.5 %all-gather.11.cloned.1.call-start = ((), (), s32[]{:S(2)}) async-start(), calls=%async_computation.6 | async-start | bytes 2621440 | tf_op jit(solution)/shard_map/all_gather | solution.py:564
  9.4 389.0 %reduce-scatter.3.cloned.1.call-start = ((), (), s32[]{:S(2)}) async-start(), calls=%async_computation.2 | async-start | bytes 3932160 | tf_op jit(solution)/shard_map/reduce_scatter | solution.py:573
  187.6 224.4 %reduce-scatter.5.cloned.1.call-start = ((), (), s32[]{:S(2)}) async-start(), calls=%async_computation.3 | async-start | bytes 11796480 | tf_op jit(solution)/shard_map/reduce_scatter | solution.py:573
  415.1 2.3 copy-start
  416.6 2.2 copy-start.1
Sparse Core Ops, SparseCore 0:
  9.5 48.0 all-gather.6
  59.2 44.2 all-gather.8
  105.1 44.2 all-gather.10
  187.8 61.3 reduce-scatter.2
  251.4 160.6 reduce-scatter.4
